TPU v7x, 32 devices: a whole 2x2x4 slice. The times are simulated.
32 devices in a mesh: col: 16 (over z, y, x), lev: 2 (over core).
Axes of the slice: x: 2, y: 2, z: 4, core: 2. Of those that a mesh axis runs over, the one named last changes fastest.
Arguments:
- perturbations: float32 [80, 16, 16384], P(None, 'lev', 'col'), may hold values from -0.625 to 0.625
- gradient: float32 [32, 16, 16384], P(None, 'lev', 'col'), may hold values from -2 to 2
- horizontal: float32 [20, 16384], P(None, 'col'), may hold values from -50 to 50
- area: float32 [16384], P('col'), may hold values from 1 to 60
- vertical: float32 [20, 16], P(None, 'lev'), may hold values from -1.25 to 1.25
Outputs:
- increment: float32 [32, 16, 16384], P(None, 'lev', 'col')
- background: float32 [32], replicated
All inputs are finite; a program needn't handle non-finite values.
Results may differ from a plain program's by a relative error of at most 0.0003.
Values sent between devices are 32-bit elements; how exact they have to be, the bound alone decides.
A program may use at most 128 MiB of HBM per device.

v0:
```python
import jax
import jax.numpy as jnp
from jax import lax
from jax.sharding import PartitionSpec as P

TOP_PRECISION = lax.Precision.HIGHEST


def adjoint_terms(perturbations, weighted, modes):
    mode_products = weighted[:, :, None, :] * modes[None, None, :, :]
    return jnp.einsum("klc,vlbc->lkvb", perturbations, mode_products, precision=TOP_PRECISION)


def project_levels(vertical, terms):
    return jnp.einsum("al,lkvb->vkab", vertical, terms, precision=TOP_PRECISION)


def mode_factor(mode_power, area_sum, count_modes):
    return 1.0 / jnp.sqrt(count_modes * (mode_power / area_sum + 1e-06))


def per_device(perturbations, gradient, horizontal, area, vertical):
    count_modes = horizontal.shape[0]
    columns = horizontal.shape[1] * lax.axis_size("col")
    power_local = jnp.sum(area[None, :] * horizontal * horizontal, axis=1)
    area_local = jnp.sum(area)
    weighted = gradient * (area * columns)[None, None, :]
    terms = adjoint_terms(perturbations, weighted, horizontal)
    summed, doubled_power, doubled = lax.psum(
        (project_levels(vertical, terms), power_local, area_local), ("col", "lev")
    )
    area_sum = doubled / lax.axis_size("lev")
    mode_power = doubled_power / lax.axis_size("lev")
    factor = mode_factor(mode_power, area_sum, count_modes)
    scaled_terms = horizontal * factor[:, None]
    control = summed * (factor / area_sum)[None, None, None, :]
    lifted = jnp.einsum("al,vkab->lkvb", vertical, control, precision=TOP_PRECISION)
    member_spread = jnp.einsum("lkvb,klc->lvbc", lifted, perturbations, precision=TOP_PRECISION)
    increment = jnp.einsum("trxa,xa->rta", member_spread, scaled_terms, precision=TOP_PRECISION)
    background = 0.5 * jnp.sum(control * control, axis=(1, 2, 3))
    return (increment, background)


def solution(mesh):
    return jax.shard_map(
        per_device,
        mesh=mesh,
        in_specs=(
            P(None, "lev", "col"),
            P(None, "lev", "col"),
            P(None, "col"),
            P("col"),
            P(None, "lev"),
        ),
        out_specs=(P(None, "lev", "col"), P()),
        check_vma=False,
    )
```

profile of v0, /device:TPU:0, one launch (start us, length us, event | category | flops | bytes accessed | tf_op | source)
XLA Modules:
  0.0 289.0 jit_solution(13503806161520612798)
XLA Ops:
  7.2 0.0 copy-start
  7.2 0.0 all-reduce.3.cloned.1.call-start
  7.2 1.4 broadcast_multiply_fusion.2
  8.7 1.3 broadcast_multiply_fusion.1
  10.0 10.6 %broadcast_multiply_fusion = f32[32,8,20,1024]{3,1,2,0:T(8,128)} fusion(f32[20,1024]{1,0:T(8,128)} %param.7, f32[32,8,1024]{2,1,0:T(8,128)S(1)} %broadcast_multiply_fusion.1), kind=kLoop, calls=%fused_computation.3 | loop fusion | flops 5242880 | bytes 22102016 | tf_op jit(solution)/shard_map/mul | solution.py:10
  20.6 0.0 copy-done
  20.6 0.0 copy-start.2
  20.6 38.6 %fusion.12 = f32[8,80,32,20]{1,2,3,0:T(8,128)S(1)} fusion(f32[80,8,1024,1]{2,1,0,3:T(8,128)S(1)} %bitcast.23, f32[32,8,20,1024]{3,1,2,0:T(8,128)} %broadcast_multiply_fusion), kind=kOutput, calls=%fused_computation.14 | convolution fusion | flops 5033164800 | bytes 25231360 | tf_op jit(solution)/shard_map/klc,vlbc->lkvb/dot_general | solution.py:11
  59.2 0.0 copy-done.2
  59.2 0.0 copy-start.1
  59.2 0.0 copy-start.3
  59.2 10.3 %convolution_bitcast_fusion = f32[32,80,20,20]{1,2,3,0:T(8,128)} fusion(f32[8,80,32,20]{1,2,3,0:T(8,128)S(1)} %fusion.12, f32[20,8]{0,1:T(8,128)S(1)} %copy-done.2), kind=kOutput, calls=%fused_computation.9 | convolution fusion | flops 98304000 | bytes 5735040 | tf_op jit(solution)/shard_map/al,lkvb->vkab/dot_general | solution.py:15
  69.5 0.0 all-reduce.3.cloned.1.call-update
  69.6 0.0 copy-done.1
  69.6 0.0 copy-done.3
  69.6 0.1 fusion.17
  69.7 43.9 %all-reduce = (f32[20]{0:T(128)S(1)}, f32[]{:T(128)}) all-reduce(f32[20]{0:T(128)S(1)} %fusion.17, f32[]{:T(128)} %get-tuple-element.7), channel_id=1, replica_groups=mesh['col'=16,'lev'=2] {'col','lev'}, use_global_device_ids=true, to_apply=%region_1.0 | all-reduce | flops 21 | bytes 168 | tf_op jit(solution)/shard_map/psum | solution.py:29
  114.3 0.1 multiply_bitcast_fusion
  114.3 132.2 %all-reduce.3.cloned.1.call-done = f32[32,80,20,20]{1,2,3,0:T(8,128)} async-done(((f32[32,80,20,20]{1,2,3,0:T(8,128)}), f32[32,80,20,20]{1,2,3,0:T(8,128)}) %all-reduce.3.cloned.1.call-update) | async-done | bytes 4096016 | tf_op jit(solution)/shard_map/psum | solution.py:29
  246.5 0.0 slice-start
  246.5 8.6 %fusion.9 = f32[8,80,32,20]{1,0,3,2:T(8,128)S(1)} fusion(f32[32,80,20,20]{1,2,3,0:T(8,128)} %all-reduce.3.cloned.1.call-done, f32[20]{0:T(128)S(1)} %get-tuple-element.4, f32[20,8]{0,1:T(8,128)S(1)} %copy-done.2), kind=kOutput, calls=%fused_computation.13 | convolution fusion | flops 99328000 | bytes 5735120 | tf_op jit(solution)/shard_map/al,vkab->lkvb/dot_general | solution.py:37
  255.2 0.0 slice-start.1
  255.2 23.4 %multiply_reduce_fusion = f32[1024,8,32]{0,2,1:T(8,128)S(1)} fusion(f32[1024,20]{0,1:T(8,128)S(1)} %multiply_bitcast_fusion, f32[8,80,32,20]{1,0,3,2:T(8,128)S(1)} %fusion.9, f32[80,8,1024,1]{2,1,0,3:T(8,128)S(1)} %bitcast.24), kind=kOutput, calls=%fused_computation | convolution fusion | flops 5043388416 | bytes 5390336 | tf_op jit(solution)/shard_map/lkvb,klc->lvbc/dot_general | solution.py:38
  278.6 1.6 copy.46
  280.2 0.0 slice-done
  280.2 0.0 slice-done.1
  280.2 1.4 multiply_reduce_fusion.1
  281.6 0.5 broadcast_multiply_fusion.3
  (2 shorter events, 0.0 us)
Async XLA Ops:
  7.2 13.4 %copy-start = (f32[80,8,1024]{2,1,0:T(8,128)S(1)}, f32[80,8,1024]{2,1,0:T(8,128)}, u32[]{:S(2)}) copy-start(f32[80,8,1024]{2,1,0:T(8,128)} %param.5) | copy-start | bytes 7864324
  7.2 239.3 %all-reduce.3.cloned.1.call-start = ((), (), s32[]{:S(2)}) async-start(), calls=%async_computation | async-start | bytes 15728640 | tf_op jit(solution)/shard_map/psum | solution.py:29
  20.6 38.6 %copy-start.2 = (f32[20,8]{0,1:T(8,128)S(1)}, f32[20,8]{0,1:T(8,128)}, u32[]{:S(2)}) copy-start(f32[20,8]{0,1:T(8,128)} %param.9) | copy-start | bytes 1924
  59.2 10.3 %copy-start.1 = (f32[20,1024]{1,0:T(8,128)S(1)}, f32[20,1024]{1,0:T(8,128)}, u32[]{:S(2)}) copy-start(f32[20,1024]{1,0:T(8,128)} %param.7) | copy-start | bytes 245764
  59.2 10.3 %copy-start.3 = (f32[1024]{0:T(1024)S(1)}, f32[1024]{0:T(1024)}, u32[]{:S(2)}) copy-start(f32[1024]{0:T(1024)} %param.8) | copy-start | bytes 12292
  246.5 33.6 %slice-start = ((s8[7864320]{0:T(1024)(128)(4,1)}), s8[4194304]{0:T(1024)(128)(4,1)S(1)}, s32[]{:S(2)}) async-start(s8[7864320]{0:T(1024)(128)(4,1)} %bitcast.25), calls=%async_computation.1 | async-start | bytes 8388608
  255.2 25.0 %slice-start.1 = ((s8[7864320]{0:T(1024)(128)(4,1)}), s8[3670016]{0:T(1024)(128)(4,1)S(1)}, s32[]{:S(2)}) async-start(s8[7864320]{0:T(1024)(128)(4,1)} %bitcast.25), calls=%async_computation.2 | async-start | bytes 7340032
Sparse Core Ops, SparseCore 0:
  69.7 176.8 all-reduce.2
where the time goes:
time: 289 us
  waiting for transfers between devices  132 us (46%)
  matrix products  80.9 us (28%)
  blocking collectives  43.9 us (15%)
  other arithmetic  15.5 us (5%)
  between operations  14.8 us (5%)
    psum x1, waiting for transfers between devices, per_device(): lax.psum((project_levels(vertical, terms), power_local, area_local), ('co...  132 us
    psum x1, blocking collectives, per_device(): lax.psum((project_levels(vertical, terms), power_local, area_local), ('co...  43.9 us
    dot_general x1, matrix products, adjoint_terms(): jnp.einsum('klc,vlbc->lkvb', perturbations, mode_products, precision=TOP_...  38.6 us
    dot_general x1, matrix products, per_device(): jnp.einsum('lkvb,klc->lvbc', lifted, perturbations, precision=TOP_PRECISION)  23.4 us
    mul x1, other arithmetic, adjoint_terms(): mode_products = weighted[:, :, None, :] * modes[None, None, :, :]  10.6 us
    dot_general x1, matrix products, project_levels(): return jnp.einsum('al,lkvb->vkab', vertical, terms, precision=TOP_PRECISION)  10.3 us
    dot_general x1, matrix products, per_device(): jnp.einsum('al,vkab->lkvb', vertical, control, precision=TOP_PRECISION)  8.63 us
  transfers between devices with their start and end apart: 1, of which 1 were waited for; matrix products, arithmetic and copies ran while one was open for 0% of the time, Pallas kernels for 0%

commit v1 on v0

--- a/solution.py
+++ b/solution.py
@@ -27,7 +27,7 @@
     weighted = gradient * (area * columns)[None, None, :]
     terms = adjoint_terms(perturbations, weighted, horizontal)
     summed, doubled_power, doubled = lax.psum(
-        (project_levels(vertical, terms), power_local, area_local), ("col", "lev")
+        lax.psum((project_levels(vertical, terms), power_local, area_local), "lev"), "col"
     )
     area_sum = doubled / lax.axis_size("lev")
     mode_power = doubled_power / lax.axis_size("lev")

time: 289 us -> 402 us (1.39)
  waiting for transfers between devices: 132 us -> 241 us
    psum x1 -> x2, waiting for transfers between devices: 132 us -> 241 us  [the longest x1 203 us: per_device(): lax.psum(lax.psum((project_levels(vertical, terms), power_local, area_loc...]
    psum x1 -> x2, blocking collectives: 43.9 us -> 47.6 us  [the longest x1 44.5 us: per_device(): lax.psum(lax.psum((project_levels(vertical, terms), power_local, area_loc...]
  transfers between devices with their start and end apart: 1 -> 2, of which waited for: 1 -> 2; matrix products, arithmetic and copies ran while one was open for 0% -> 0% of each run, Pallas kernels for 0% -> 0%
where the time goes in v1:
time: 402 us
  waiting for transfers between devices  241 us (60%)
  matrix products  81.2 us (20%)
  blocking collectives  47.6 us (12%)
  other arithmetic  15.5 us (4%)
  between operations  14.8 us (4%)
    psum x1, waiting for transfers between devices, per_device(): lax.psum(lax.psum((project_levels(vertical, terms), power_local, area_loc...  203 us
    psum x1, blocking collectives, per_device(): lax.psum(lax.psum((project_levels(vertical, terms), power_local, area_loc...  44.5 us
    dot_general x1, matrix products, adjoint_terms(): jnp.einsum('klc,vlbc->lkvb', perturbations, mode_products, precision=TOP_...  38.6 us
    psum x1, waiting for transfers between devices, per_device(): lax.psum((project_levels(vertical, terms), power_local, area_local), 'lev')  38 us
    dot_general x1, matrix products, per_device(): jnp.einsum('lkvb,klc->lvbc', lifted, perturbations, precision=TOP_PRECISION)  23.4 us
    mul x1, other arithmetic, adjoint_terms(): mode_products = weighted[:, :, None, :] * modes[None, None, :, :]  10.6 us
    dot_general x1, matrix products, project_levels(): return jnp.einsum('al,lkvb->vkab', vertical, terms, precision=TOP_PRECISION)  10.3 us
    dot_general x1, matrix products, per_device(): jnp.einsum('al,vkab->lkvb', vertical, control, precision=TOP_PRECISION)  8.87 us
  transfers between devices with their start and end apart: 2, of which 2 were waited for; matrix products, arithmetic and copies ran while one was open for 0% of the time, Pallas kernels for 0%

profile of v1, /device:TPU:0, one launch (start us, length us, event | category | flops | bytes accessed | tf_op | source)
XLA Modules:
  0.0 402.0 jit_solution(254839177862882139)
XLA Ops:
  7.2 0.0 copy-start
  7.2 0.0 all-reduce.5.cloned.1.call-start
  7.2 1.4 broadcast_multiply_fusion.2
  8.7 1.3 broadcast_multiply_fusion.1
  10.0 10.6 %broadcast_multiply_fusion = f32[32,8,20,1024]{3,1,2,0:T(8,128)} fusion(f32[20,1024]{1,0:T(8,128)} %param.7, f32[32,8,1024]{2,1,0:T(8,128)S(1)} %broadcast_multiply_fusion.1), kind=kLoop, calls=%fused_computation.3 | loop fusion | flops 5242880 | bytes 22102016 | tf_op jit(solution)/shard_map/mul | solution.py:10
  20.6 0.0 copy-done
  20.6 0.0 copy-start.2
  20.6 38.6 %fusion.12 = f32[8,80,32,20]{1,2,3,0:T(8,128)S(1)} fusion(f32[80,8,1024,1]{2,1,0,3:T(8,128)S(1)} %bitcast.23, f32[32,8,20,1024]{3,1,2,0:T(8,128)} %broadcast_multiply_fusion), kind=kOutput, calls=%fused_computation.14 | convolution fusion | flops 5033164800 | bytes 25231360 | tf_op jit(solution)/shard_map/klc,vlbc->lkvb/dot_general | solution.py:11
  59.2 0.0 copy-done.2
  59.2 10.3 %convolution_bitcast_fusion = f32[32,80,20,20]{1,2,3,0:T(8,128)} fusion(f32[8,80,32,20]{1,2,3,0:T(8,128)S(1)} %fusion.12, f32[20,8]{0,1:T(8,128)S(1)} %copy-done.2), kind=kOutput, calls=%fused_computation.9 | convolution fusion | flops 98304000 | bytes 5735040 | tf_op jit(solution)/shard_map/al,lkvb->vkab/dot_general | solution.py:15
  69.5 0.0 copy-start.1
  69.5 0.0 copy-start.3
  69.5 0.0 all-reduce.5.cloned.1.call-update
  69.5 0.0 all-reduce.7.cloned.1.call-start
  69.6 38.0 %all-reduce.5.cloned.1.call-done = f32[32,80,20,20]{1,2,3,0:T(8,128)} async-done(((f32[32,80,20,20]{1,2,3,0:T(8,128)}), f32[32,80,20,20]{1,2,3,0:T(8,128)}) %all-reduce.5.cloned.1.call-update) | async-done | bytes 4096016 | tf_op jit(solution)/shard_map/psum | solution.py:30
  107.6 0.0 all-reduce.7.cloned.1.call-update
  107.6 0.0 copy-done.1
  107.6 0.0 copy-done.3
  107.7 0.1 fusion.17
  107.8 3.1 all-reduce.1
  110.9 44.5 %all-reduce = (f32[20]{0:T(128)S(1)}, f32[]{:T(128)}) all-reduce(f32[20]{0:T(128)S(1)} %get-tuple-element.4, f32[]{:T(128)} %get-tuple-element.5), channel_id=1, replica_groups=mesh['col'=16,'lev'=2] {'col'}, use_global_device_ids=true, to_apply=%region_2.0 | all-reduce | flops 21 | bytes 168 | tf_op jit(solution)/shard_map/psum | solution.py:29
  156.0 0.1 multiply_bitcast_fusion
  156.1 203.3 %all-reduce.7.cloned.1.call-done = f32[32,80,20,20]{1,2,3,0:T(8,128)} async-done(((f32[32,80,20,20]{1,2,3,0:T(8,128)}), f32[32,80,20,20]{1,2,3,0:T(8,128)}) %all-reduce.7.cloned.1.call-update) | async-done | bytes 4096016 | tf_op jit(solution)/shard_map/psum | solution.py:29
  359.4 0.0 slice-start
  359.4 8.9 %fusion.9 = f32[8,80,32,20]{1,0,3,2:T(8,128)S(1)} fusion(f32[32,80,20,20]{1,2,3,0:T(8,128)} %all-reduce.7.cloned.1.call-done, f32[20]{0:T(128)S(1)} %get-tuple-element.6, f32[20,8]{0,1:T(8,128)S(1)} %copy-done.2), kind=kOutput, calls=%fused_computation.13 | convolution fusion | flops 99328000 | bytes 5735120 | tf_op jit(solution)/shard_map/al,vkab->lkvb/dot_general | solution.py:37
  368.3 0.0 slice-start.1
  368.3 23.4 %multiply_reduce_fusion = f32[1024,8,32]{0,2,1:T(8,128)S(1)} fusion(f32[1024,20]{0,1:T(8,128)S(1)} %multiply_bitcast_fusion, f32[8,80,32,20]{1,0,3,2:T(8,128)S(1)} %fusion.9, f32[80,8,1024,1]{2,1,0,3:T(8,128)S(1)} %bitcast.24), kind=kOutput, calls=%fused_computation | convolution fusion | flops 5043388416 | bytes 5390336 | tf_op jit(solution)/shard_map/lkvb,klc->lvbc/dot_general | solution.py:38
  391.7 1.6 copy.46
  393.2 0.0 slice-done
  393.2 0.0 slice-done.1
  393.3 1.4 multiply_reduce_fusion.1
  394.7 0.5 broadcast_multiply_fusion.3
  (2 shorter events, 0.0 us)
Async XLA Ops:
  7.2 13.4 %copy-start = (f32[80,8,1024]{2,1,0:T(8,128)S(1)}, f32[80,8,1024]{2,1,0:T(8,128)}, u32[]{:S(2)}) copy-start(f32[80,8,1024]{2,1,0:T(8,128)} %param.5) | copy-start | bytes 7864324
  7.2 100.4 %all-reduce.5.cloned.1.call-start = ((), (), s32[]{:S(2)}) async-start(), calls=%async_computation | async-start | bytes 15728640 | tf_op jit(solution)/shard_map/psum | solution.py:30
  20.6 38.6 %copy-start.2 = (f32[20,8]{0,1:T(8,128)S(1)}, f32[20,8]{0,1:T(8,128)}, u32[]{:S(2)}) copy-start(f32[20,8]{0,1:T(8,128)} %param.9) | copy-start | bytes 1924
  69.5 38.1 %copy-start.1 = (f32[20,1024]{1,0:T(8,128)S(1)}, f32[20,1024]{1,0:T(8,128)}, u32[]{:S(2)}) copy-start(f32[20,1024]{1,0:T(8,128)} %param.7) | copy-start | bytes 245764
  69.5 38.1 %copy-start.3 = (f32[1024]{0:T(1024)S(1)}, f32[1024]{0:T(1024)}, u32[]{:S(2)}) copy-start(f32[1024]{0:T(1024)} %param.8) | copy-start | bytes 12292
  69.5 289.8 %all-reduce.7.cloned.1.call-start = ((), (), s32[]{:S(2)}) async-start(), calls=%async_computation.1 | async-start | bytes 15728640 | tf_op jit(solution)/shard_map/psum | solution.py:29
  359.4 33.9 %slice-start = ((s8[7864320]{0:T(1024)(128)(4,1)}), s8[4194304]{0:T(1024)(128)(4,1)S(1)}, s32[]{:S(2)}) async-start(s8[7864320]{0:T(1024)(128)(4,1)} %bitcast.25), calls=%async_computation.2 | async-start | bytes 8388608
  368.3 25.0 %slice-start.1 = ((s8[7864320]{0:T(1024)(128)(4,1)}), s8[3670016]{0:T(1024)(128)(4,1)S(1)}, s32[]{:S(2)}) async-start(s8[7864320]{0:T(1024)(128)(4,1)} %bitcast.25), calls=%async_computation.3 | async-start | bytes 7340032
Sparse Core Ops, SparseCore 0:
  69.7 37.9 all-reduce.4
  113.8 245.5 all-reduce.6
